TPU v7x, 256 devices: a 8x8x2 block of a 8x8x16 slice. The times are simulated.
256 devices in a mesh: img: 2 (over z), ga: 16 (over y, core), band: 8 (over x).
Axes of the slice: x: 8, y: 8, z: 2, core: 2. Of those that a mesh axis runs over, the one named last changes fastest.
The devices are a block of a 8x8x16 slice.
Arguments:
- orbitals: bfloat16 [1536, 49152], P(('img', 'band'), 'ga'), parts along dimension 0, as said below
- kernel: float32 [49152], P('ga'), may hold values from 0.3 to 3
- block_vectors: bfloat16 [512, 49152], P(('img', 'band'), 'ga'), parts along dimension 0
Outputs:
- ace_vectors: bfloat16 [1536, 49152], P(('img', 'band'), 'ga'), parts along dimension 0
- exchange_block: bfloat16 [512, 49152], P(('img', 'band'), 'ga'), parts along dimension 0
There are 2 independent parts, one for each index of `img`. A program takes and returns all parts, laid end to end along the dimension named above; an argument that names none is the same for every part. Nothing has to cross between parts.
Inputs may be any that keep to these rules, and one draw needn't show every extreme that they name: `orbitals`: the bands of one image are linearly independent, and the block lies largely in their span.
All inputs are finite; a program needn't handle non-finite values.
Results may differ from a plain program's by a relative error of at most 0.02.
Values may be sent and summed in bfloat16 or wider, within the bound.
A program may use at most 64 MiB of HBM per device.

v0:
```python
import jax
import jax.numpy as jnp
from jax import lax
from jax.sharding import PartitionSpec as P


def over_pieces(shard, axis):
    pieces = lax.all_gather(shard, axis).astype(jnp.float32)
    return pieces.sum(axis=0)


def from_everyone(shard, axis):
    count = lax.axis_size(axis)
    return lax.all_to_all(
        jnp.broadcast_to(shard[None], (count, *shard.shape)), axis, 0, 0, tiled=True
    )


def in_order(pieces, dim):
    pieces = jnp.moveaxis(pieces, 0, dim)
    dims = pieces.shape
    return pieces.reshape(*dims[:dim], dims[dim] * dims[dim + 1], *dims[dim + 2 :])


def gathered_copies(shard, axis, dim):
    pieces = from_everyone(shard, axis)
    return in_order(pieces, dim)


def taken_together(shard, axis):
    return from_everyone(shard, axis).astype(jnp.float32).sum(axis=0)


def cut_along(shard, dim, count):
    dims = shard.shape
    pieces = shard.reshape(*dims[:dim], count, dims[dim] // count, *dims[dim + 1 :])
    return jnp.moveaxis(pieces, dim, 0)


def sent_and_summed(shard, axis, dim):
    pieces = cut_along(shard, dim, lax.axis_size(axis))
    arrived = lax.all_to_all(pieces, axis, split_axis=0, concat_axis=0, tiled=True)
    return arrived.astype(jnp.float32).sum(axis=0)


def contract_first(left, right):
    return lax.dot_general(left, right, (((0,), (0,)), ((), ())), precision=lax.Precision.HIGHEST)


def shards(orbitals, kernel, block_vectors):
    groups = lax.axis_size("ga")
    own_band = lax.axis_index("band")
    total_coeffs = orbitals.shape[1] * groups
    full_orbitals, full_block = (
        lax.all_gather(orbitals, "band", axis=0, tiled=True),
        lax.all_gather(block_vectors, "band", axis=0, tiled=True),
    )
    weighted = (-(full_orbitals.astype(jnp.float32) * kernel[None, :])).astype(jnp.bfloat16)
    own_rows = orbitals.shape[0]
    partial_rows = lax.dot_general(
        orbitals, weighted, (((1,), (1,)), ((), ())), preferred_element_type=jnp.float32
    )
    summed_rows = over_pieces(partial_rows.astype(jnp.bfloat16), "ga").astype(jnp.float32)
    margin = (
        -gathered_copies(summed_rows.astype(jnp.bfloat16), "band", 0).astype(summed_rows.dtype)
        / total_coeffs
    )
    factor = jnp.linalg.cholesky(margin)
    identity = jnp.eye(factor.shape[0], dtype=jnp.float32)
    inverse = lax.linalg.triangular_solve(factor, identity, left_side=True, lower=True)
    inverse_rows = lax.dynamic_slice_in_dim(inverse, own_band * own_rows, own_rows, 0)
    projector = jnp.dot(inverse_rows, weighted.astype(jnp.float32), precision=lax.Precision.HIGHEST)
    local_coupling = jnp.dot(
        projector, full_block.astype(jnp.float32).T, precision=lax.Precision.HIGHEST
    )
    coupling = (
        taken_together(local_coupling.astype(jnp.bfloat16), "ga").astype(jnp.float32) / total_coeffs
    )
    applied = sent_and_summed(
        (-contract_first(coupling, projector)).astype(jnp.bfloat16), "band", 0
    )
    return (projector.astype(jnp.bfloat16), applied.astype(jnp.bfloat16))


def solution(mesh):
    placed = (P(("img", "band"), "ga"), P("ga"), P(("img", "band"), "ga"))
    return jax.shard_map(
        shards,
        mesh=mesh,
        in_specs=placed,
        out_specs=(P(("img", "band"), "ga"), P(("img", "band"), "ga")),
        check_vma=False,
    )
```

profile of v0, /device:TPU:513, one launch (start us, length us, event | category | flops | bytes accessed | tf_op | source)
XLA Modules:
  0.0 510.5 jit_solution(14080767505893318742)
XLA Ops:
  8.0 80.9 %all-gather.5.cloned.1.call-done = bf16[768,3072]{1,0:T(8,128)(2,1)} async-done(((bf16[96,3072]{1,0:T(8,128)(2,1)}), bf16[768,3072]{1,0:T(8,128)(2,1)}) %all-gather.5.cloned.1.call-update) | async-done | bytes 4718608 | tf_op jit(solution)/shard_map/all_gather | solution.py:55
  89.0 4.7 fusion.21
  93.8 41.2 %all-gather.9.cloned.1.call-done = bf16[1536,768]{1,0:T(8,128)(2,1)} async-done(((bf16[96,768]{1,0:T(8,128)(2,1)}), bf16[1536,768]{1,0:T(8,128)(2,1)}) %all-gather.9.cloned.1.call-update) | async-done | bytes 2359312 | tf_op jit(solution)/shard_map/all_gather | solution.py:8
  138.0 6.4 %all-to-all-start = ((bf16[8,96,768]{2,1,0:T(8,128)(2,1)}), bf16[8,96,768]{2,1,0:T(8,128)(2,1)S(1)}, u32[]{:S(2)}, u32[]{:S(2)}) async-start(bf16[8,96,768]{2,1,0:T(8,128)(2,1)} %broadcast_in_dim.5), calls=%async_computation | async-start | bytes 2359296 | tf_op jit(solution)/shard_map/all_to_all | solution.py:14
  147.9 35.2 %all-to-all-done = bf16[8,96,768]{2,1,0:T(8,128)(2,1)S(1)} async-done(((bf16[8,96,768]{2,1,0:T(8,128)(2,1)}), bf16[8,96,768]{2,1,0:T(8,128)(2,1)S(1)}, u32[]{:S(2)}, u32[]{:S(2)}) %all-to-all-start) | async-done | bytes 1179680 | tf_op jit(solution)/shard_map/all_to_all | solution.py:14
  189.2 11.7 %cholesky.165 = f32[128,128]{1,0:T(8,128)S(1)} custom-call(f32[128,128]{1,0:T(8,128)S(1)} %cholesky.424), custom_call_target="Cholesky" | custom-call | tf_op jit(solution)/shard_map/jit(cholesky)/cholesky | solution.py:68
  201.0 9.8 %custom-call.46 = f32[1,128,128]{1,2,0:T(8,128)S(1)} custom-call(f32[1,128,128]{2,1,0:T(8,128)S(1)} %get-tuple-element.45), custom_call_target="InvertDiagBlocksLowerTriangular" | custom-call | tf_op jit(solution)/shard_map/jit(cholesky)/cholesky | solution.py:68
  213.8 11.7 %cholesky.188 = f32[128,128]{1,0:T(8,128)S(1)} custom-call(f32[128,128]{1,0:T(8,128)S(1)} %cholesky.428), custom_call_target="Cholesky" | custom-call | tf_op jit(solution)/shard_map/jit(cholesky)/cholesky | solution.py:68
  225.5 10.0 %custom-call.47 = f32[1,128,128]{1,2,0:T(8,128)S(1)} custom-call(f32[1,128,128]{2,1,0:T(8,128)S(1)} %get-tuple-element.42), custom_call_target="InvertDiagBlocksLowerTriangular" | custom-call | tf_op jit(solution)/shard_map/jit(cholesky)/cholesky | solution.py:68
  237.4 11.7 %cholesky.354 = f32[128,128]{1,0:T(8,128)S(1)} custom-call(f32[128,128]{1,0:T(8,128)S(1)} %cholesky.433), custom_call_target="Cholesky" | custom-call | tf_op jit(solution)/shard_map/jit(cholesky)/cholesky | solution.py:68
  249.9 9.8 %custom-call.48 = f32[1,128,128]{1,2,0:T(8,128)S(1)} custom-call(f32[1,128,128]{2,1,0:T(8,128)S(1)} %get-tuple-element.39), custom_call_target="InvertDiagBlocksLowerTriangular" | custom-call | tf_op jit(solution)/shard_map/jit(cholesky)/cholesky | solution.py:68
  261.6 12.1 %cholesky.373 = f32[128,128]{1,0:T(8,128)S(1)} custom-call(f32[128,128]{1,0:T(8,128)S(1)} %cholesky.438), custom_call_target="Cholesky" | custom-call | tf_op jit(solution)/shard_map/jit(cholesky)/cholesky | solution.py:68
  274.4 9.8 %custom-call.49 = f32[1,128,128]{1,2,0:T(8,128)S(1)} custom-call(f32[1,128,128]{2,1,0:T(8,128)S(1)} %get-tuple-element.36), custom_call_target="InvertDiagBlocksLowerTriangular" | custom-call | tf_op jit(solution)/shard_map/jit(cholesky)/cholesky | solution.py:68
  286.0 11.7 %cholesky.392 = f32[128,128]{1,0:T(8,128)S(1)} custom-call(f32[128,128]{1,0:T(8,128)S(1)} %cholesky.443), custom_call_target="Cholesky" | custom-call | tf_op jit(solution)/shard_map/jit(cholesky)/cholesky | solution.py:68
  298.4 9.8 %custom-call.50 = f32[1,128,128]{1,2,0:T(8,128)S(1)} custom-call(f32[1,128,128]{2,1,0:T(8,128)S(1)} %get-tuple-element.33), custom_call_target="InvertDiagBlocksLowerTriangular" | custom-call | tf_op jit(solution)/shard_map/jit(cholesky)/cholesky | solution.py:68
  309.8 11.9 %cholesky.410 = f32[128,128]{1,0:T(8,128)S(1)} custom-call(f32[128,128]{1,0:T(8,128)S(1)} %convolution_subtract_fusion.8), custom_call_target="Cholesky" | custom-call | tf_op jit(solution)/shard_map/jit(cholesky)/cholesky | solution.py:68
  328.4 21.5 %while.1 = (s32[]{:T(128)}, f32[768,768]{1,0:T(8,128)}, s32[6,2]{0,1:T(2,128)S(1)}, f32[6,128,128]{2,1,0:T(8,128)}, s32[]{:T(128)}) while((s32[]{:T(128)}, f32[768,768]{1,0:T(8,128)}, s32[6,2]{0,1:T(2,128)S(1)}, f32[6,128,128]{2,1,0:T(8,128)}, s32[]{:T(128)}) %tuple.45), condition=%wide.while_cond, body=%wide.while_body.sunk | while | flops 2 | bytes 132705 | solution.py:70
  329.1 2.9 bitcast_dynamic-update-slice_fusion.2
  332.7 2.9 bitcast_dynamic-update-slice_fusion.2
  349.9 59.8 %custom-call.51 = f32[6,128,128]{1,2,0:T(8,128)S(1)} custom-call(f32[6,128,128]{2,1,0:T(8,128)} %get-tuple-element.9), custom_call_target="InvertDiagBlocksLowerTriangular" | custom-call | tf_op jit(solution)/shard_map/triangular_solve | solution.py:70
  422.9 3.7 fusion.65
  426.6 3.0 convolution_convert_fusion
  429.7 27.3 %all_to_all.15 = bf16[16,96,256]{2,1,0:T(8,128)(2,1)S(1)} all-to-all(bf16[16,96,256]{2,1,0:T(8,128)(2,1)S(1)} %broadcast_in_dim.7), channel_id=1, replica_groups=mesh['img'=2,'ga'=16,'band'=8] {'ga'}, dimensions={0} | all-to-all | bytes 1572864 | tf_op jit(solution)/shard_map/all_to_all | solution.py:14
  459.9 43.0 %all_to_all.16 = bf16[8,32,3072]{2,1,0:T(8,128)(2,1)S(1)} all-to-all(bf16[8,32,3072]{2,1,0:T(8,128)(2,1)S(1)} %bitcast.88), channel_id=1, replica_groups=mesh['img'=2,'ga'=16,'band'=8] {'band'}, dimensions={0} | all-to-all | bytes 3145728 | tf_op jit(solution)/shard_map/all_to_all | solution.py:42
  (87 shorter events, 61.3 us)
Async XLA Ops:
  7.2 81.8 %all-gather.5.cloned.1.call-start = ((), (), s32[]{:S(2)}) async-start(), calls=%async_computation.3 | async-start | bytes 5308416 | tf_op jit(solution)/shard_map/all_gather | solution.py:55
  8.0 127.0 %all-gather.9.cloned.1.call-start = ((), (), s32[]{:S(2)}) async-start(), calls=%async_computation.5 | async-start | bytes 2506752 | tf_op jit(solution)/shard_map/all_gather | solution.py:8
  138.0 45.0 %all-to-all-start = ((bf16[8,96,768]{2,1,0:T(8,128)(2,1)}), bf16[8,96,768]{2,1,0:T(8,128)(2,1)S(1)}, u32[]{:S(2)}, u32[]{:S(2)}) async-start(bf16[8,96,768]{2,1,0:T(8,128)(2,1)} %broadcast_in_dim.5), calls=%async_computation | async-start | bytes 2359296 | tf_op jit(solution)/shard_map/all_to_all | solution.py:14
  144.5 282.2 %all-gather.7.cloned.1.call-start = ((), (), s32[]{:S(2)}) async-start(), calls=%async_computation.4 | async-start | bytes 1769472 | tf_op jit(solution)/shard_map/all_gather | solution.py:56
  187.8 1.5 copy-start.1
  328.4 84.5 %copy-start = (f32[768,768]{1,0:T(8,128)S(1)}, f32[768,768]{1,0:T(8,128)}, u32[]{:S(2)}) copy-start(f32[768,768]{1,0:T(8,128)} %fusion.25) | copy-start | bytes 7077892
  415.0 7.9 %slice-start = ((s8[4718592]{0:T(1024)(128)(4,1)}), s8[4194304]{0:T(1024)(128)(4,1)S(1)}, s32[]{:S(2)}) async-start(s8[4718592]{0:T(1024)(128)(4,1)} %bitcast.90), calls=%async_computation.6 | async-start | bytes 8388608
  417.5 5.4 %slice-start.1 = ((s8[4718592]{0:T(1024)(128)(4,1)}), s8[524288]{0:T(1024)(128)(4,1)S(1)}, s32[]{:S(2)}) async-start(s8[4718592]{0:T(1024)(128)(4,1)} %bitcast.90), calls=%async_computation.7 | async-start | bytes 1048576
  419.5 3.4 copy-start.2
Sparse Core Ops, SparseCore 0:
  9.8 79.1 all-gather.4
  93.9 40.9 all-gather.8
  147.1 44.9 all-gather.6
where the time goes:
time: 515 us; the launch traced here: 511 us
  other arithmetic  193 us (37%)
  waiting for transfers between devices  159 us (31%)
  blocking collectives  70.3 us (14%)
  matrix products  37 us (7%)
  local copies, waits for them, and re-layouts  26.8 us (5%)
  between operations  18.2 us (4%)
  starting transfers between devices  6.6 us (1%)
    another operation x22, other arithmetic, shards(): factor = jnp.linalg.cholesky(margin)  124 us
    all_gather x1, waiting for transfers between devices, shards(): lax.all_gather(orbitals, 'band', axis=0, tiled=True)  80.9 us
    another operation x3, other arithmetic, shards(): lax.linalg.triangular_solve(factor, identity, left_side=True, lower=True)  61.4 us
    all_to_all x1, blocking collectives, sent_and_summed(): lax.all_to_all(pieces, axis, split_axis=0, concat_axis=0, tiled=True)  43 us
    all_gather x1, waiting for transfers between devices, over_pieces(): pieces = lax.all_gather(shard, axis).astype(jnp.float32)  41.2 us
    all_to_all x1, waiting for transfers between devices, from_everyone(): lax.all_to_all(jnp.broadcast_to(shard[None], (count, *shard.shape)), axis...  35.2 us
    all_to_all x1, blocking collectives, from_everyone(): lax.all_to_all(jnp.broadcast_to(shard[None], (count, *shard.shape)), axis...  27.3 us
    another operation x18, local copies, waits for them, and re-layouts  21.5 us
  transfers between devices with their start and end apart: 4, of which 3 were waited for; matrix products, arithmetic and copies ran while one was open for 47% of the time, Pallas kernels for 0%

commit v1 on v0

v1 whole, which is shorter than its diff:
```python
import functools
import jax
import jax.numpy as jnp
from jax import lax
from jax.experimental import pallas as pl
from jax.experimental.pallas import tpu as pltpu
from jax.sharding import PartitionSpec as P

LANES = 128
SUB = 8
TILE = 128
CORES = 2
MESH = pl.DeviceIdType.MESH
F32 = jnp.float32
BF16 = jnp.bfloat16
VMEM = pl.BlockSpec(memory_space=pltpu.VMEM)


def row_of(value, index):
    return jnp.broadcast_to(value[index : index + 1, :], value.shape)


def column_of(value, index):
    return jnp.broadcast_to(value[:, index : index + 1], value.shape)


def inverse_factor(rows):
    sub = lax.broadcasted_iota(jnp.int32, (SUB, LANES), 0)
    lane = lax.broadcasted_iota(jnp.int32, (SUB, LANES), 1)
    rows = list(rows)
    count = len(rows)
    done = []
    for t in range(count):
        first = t * SUB
        inside = (lane >= first) & (lane < first + SUB)
        strip = rows[t]
        columns = [column_of(strip, first + k) for k in range(SUB)]
        strip = jnp.where(inside, jnp.where(lane - first == sub, 1.0, 0.0), strip)
        forward = strip
        scale = jnp.ones((SUB, LANES), F32)
        for j in range(SUB):
            pivot = 1.0 / row_of(columns[j], j)
            scale = jnp.where(sub == j, pivot, scale)
            factor = jnp.where(sub == j, 0.0, columns[j] * pivot)
            for k in range(j + 1, SUB):
                columns[k] = columns[k] - factor * row_of(columns[k], j)
            strip = strip - factor * row_of(strip, j)
            if j < SUB - 1:
                forward = forward - jnp.where(sub > j, factor, 0.0) * row_of(forward, j)
        done.append(jnp.where(lane < first + SUB, forward * jnp.sqrt(scale), 0.0))
        if t == count - 1:
            break
        solved = strip * scale
        solved_rows = [row_of(solved, j) for j in range(SUB)]
        for r in range(t + 1, count):
            old = rows[r]
            total = jnp.where(inside, 0.0, old)
            terms = [column_of(old, first + j) * solved_rows[j] for j in range(SUB)]
            while len(terms) > 1:
                terms = [terms[i] + terms[i + 1] for i in range(0, len(terms), 2)]
            rows[r] = total - terms[0]
    return done


def split(value):
    high = value.astype(BF16)
    return high, (value - high.astype(F32)).astype(BF16)


def dot(left, right):
    return lax.dot_general(left, right, (((1,), (0,)), ((), ())), preferred_element_type=F32)


def dot_rows(left, right):
    return lax.dot_general(left, right, (((1,), (1,)), ((), ())), preferred_element_type=F32)


def dot_split(left, right):
    (lh, ll), (rh, rl) = left, right
    return dot(lh, rh) + dot(lh, rl) + dot(ll, rh)


def blocks_of(bands, vectors):
    tiles = bands // TILE
    margin = [(i, j) for i in range(tiles) for j in range(i, tiles)]
    overlap = [(i, j) for i in range(tiles) for j in range(vectors // TILE)]
    where_margin = {ij: n * TILE for n, ij in enumerate(margin)}
    where_overlap = {ij: (len(margin) + n) * TILE for n, ij in enumerate(overlap)}
    return where_margin, where_overlap, (len(margin) + len(overlap)) * TILE


def solve_kernel(bands, vectors, packed_ref, weighted_ref, ace_ref, exchange_ref, work):
    width = weighted_ref.shape[1]
    tiles = bands // TILE
    where_margin, where_overlap, _ = blocks_of(bands, vectors)
    for (i, j), row in where_margin.items():
        work[pl.ds(i * TILE, TILE), pl.ds(j * TILE, TILE)] = packed_ref[pl.ds(row, TILE), :].astype(F32)
    for (i, j), row in where_overlap.items():
        work[pl.ds(i * TILE, TILE), pl.ds(bands + j * TILE, TILE)] = packed_ref[
            pl.ds(row, TILE), :
        ].astype(F32)
    for i in range(tiles):
        work[pl.ds(i * TILE, TILE), pl.ds(bands + vectors, width)] = weighted_ref[
            pl.ds(i * TILE, TILE), :
        ].astype(F32)
    applied = None
    for k in range(tiles):
        top = k * TILE
        strips = [work[pl.ds(top + SUB * t, SUB), pl.ds(top, TILE)] for t in range(TILE // SUB)]
        inverse = jnp.concatenate(inverse_factor(strips), axis=0)
        first = top + TILE
        rest = work[pl.ds(top, TILE), pl.ds(first, work.shape[1] - first)]
        upper = dot_split(split(inverse), split(rest))
        parts = split(upper)
        for i in range(k + 1, tiles):
            at = i * TILE - first
            lower = split(upper[:, at : at + TILE].T)
            cut = tuple(part[:, at:] for part in parts)
            rows = pl.ds(i * TILE, TILE)
            cols = pl.ds(i * TILE, work.shape[1] - i * TILE)
            work[rows, cols] = work[rows, cols] - dot_split(lower, cut)
        base = bands - first
        coupling = split(upper[:, base : base + vectors].T)
        projector = tuple(part[:, base + vectors :] for part in parts)
        ace_ref[pl.ds(top, TILE), :] = upper[:, base + vectors :].astype(BF16)
        term = dot_split(coupling, projector)
        applied = term if applied is None else applied + term
    exchange_ref[...] = (-applied).astype(BF16)


def solve(packed, weighted, bands, vectors):
    width = weighted.shape[1]
    return pl.pallas_call(
        functools.partial(solve_kernel, bands, vectors),
        out_shape=(
            jax.ShapeDtypeStruct((bands, width), BF16),
            jax.ShapeDtypeStruct((vectors, width), BF16),
        ),
        in_specs=[VMEM, VMEM],
        out_specs=(VMEM, VMEM),
        scratch_shapes=[pltpu.VMEM((bands, bands + vectors + width), F32)],
        compiler_params=pltpu.CompilerParams(vmem_limit_bytes=40 * 2**20),
        name="solve",
    )(packed, weighted)


def remote(src, dst, send, recv, band, ga):
    return pltpu.make_async_remote_copy(
        src_ref=src,
        dst_ref=dst,
        send_sem=send,
        recv_sem=recv,
        device_id={"band": band, "ga": ga},
        device_id_type=MESH,
    )


def meet(devices):
    barrier = pltpu.get_barrier_semaphore()
    for band, ga in devices:
        pl.semaphore_signal(barrier, inc=1, device_id={"band": band, "ga": ga}, device_id_type=MESH)
    pl.semaphore_wait(barrier, len(devices))


def aligned(start, step, size):
    return pl.ds(pl.multiple_of(start, step), size)


def front_kernel(
    count, groups, total, orbitals_ref, block_ref, kernel_ref, packed_ref, weighted_ref,
    bands, vectors, part, half_in, half, first_in, own, second_in,
    to_bands, from_bands, to_vectors, from_vectors, pair_send, pair_recv,
    first_send, first_recv, second_send, second_recv,
    spread_send, spread_recv, give_send, give_recv,
):
    band, ga = lax.axis_index("band"), lax.axis_index("ga")
    line, core = ga // CORES, ga % CORES
    rows, cols = orbitals_ref.shape[0], weighted_ref.shape[1]
    block_rows = block_ref.shape[0]
    here = (1 - core) * band + core * line
    there = (1 - core) * line + core * band

    def along_first(q):
        return (1 - core) * q + core * band, CORES * ((1 - core) * line + core * q) + core

    def along_second(q):
        return (1 - core) * band + core * q, CORES * ((1 - core) * q + core * line) + core

    pair = (band, CORES * line + 1 - core)
    steps = range(1, count)
    meet(
        [along_first((here + d) % count) for d in steps]
        + [along_second((there + d) % count) for d in steps]
        + [pair]
    )

    moved = []
    for d in steps:
        peer = (band + d) % count
        mine = aligned(peer * cols, LANES, cols)
        moved.append((
            remote(orbitals_ref.at[:, mine], bands.at[aligned(band * rows, 16, rows), :],
                   to_bands.at[d - 1], from_bands.at[d - 1], peer, ga),
            remote(block_ref.at[:, mine], vectors.at[aligned(band * block_rows, 16, block_rows), :],
                   to_vectors.at[d - 1], from_vectors.at[d - 1], peer, ga),
        ))
    for orbital_copy, _ in moved:
        orbital_copy.start()
    for _, block_copy in moved:
        block_copy.start()
    mine = aligned(band * cols, LANES, cols)
    bands[aligned(band * rows, 16, rows), :] = orbitals_ref[:, mine]
    vectors[aligned(band * block_rows, 16, block_rows), :] = block_ref[:, mine]
    gains = kernel_ref[:, mine]
    for orbital_copy, _ in moved:
        orbital_copy.wait()

    all_rows, all_vectors = bands.shape[0], vectors.shape[0]
    tiles = all_rows // TILE
    where_margin, where_overlap, used = blocks_of(all_rows, all_vectors)
    for i in range(tiles):
        at = pl.ds(i * TILE, TILE)
        weighted_ref[at, :] = (-(bands[at, :].astype(F32) * gains)).astype(BF16)
    for i in range(tiles):
        at, after = pl.ds(i * TILE, TILE), pl.ds(i * TILE, all_rows - i * TILE)
        sums = dot_rows(bands[at, :], weighted_ref[after, :]) + dot_rows(weighted_ref[at, :], bands[after, :])
        sums = (sums * (-0.5 / total)).astype(BF16)
        for j in range(i, tiles):
            part[pl.ds(where_margin[i, j], TILE), :] = sums[:, (j - i) * TILE : (j - i + 1) * TILE]
    for _, block_copy in moved:
        block_copy.wait()
    for i in range(tiles):
        sums = dot_rows(weighted_ref[pl.ds(i * TILE, TILE), :], vectors[...])
        sums = (sums * (1.0 / total)).astype(BF16)
        for j in range(all_vectors // TILE):
            part[pl.ds(where_overlap[i, j], TILE), :] = sums[:, j * TILE : (j + 1) * TILE]
    if used < part.shape[0]:
        part[used:, :] = jnp.zeros((part.shape[0] - used, LANES), BF16)

    piece = part.shape[0] // (CORES * count)
    size = piece * count

    def piece_at(core_of, q):
        return aligned((core_of * count + q) * piece, 16, piece)

    swap = remote(part.at[aligned((1 - core) * size, 16, size), :], half_in, pair_send, pair_recv, *pair)
    swap.start()
    swap.wait()

    first = []
    for d in range(1, count + 1):
        q = (here + d) % count
        there_in = half_in[aligned(q * piece, 16, piece), :].astype(F32)
        summed = (part[piece_at(core, q), :].astype(F32) + there_in).astype(BF16)
        if d < count:
            half[d - 1] = summed
            copy = remote(half.at[d - 1], first_in.at[d - 1], first_send.at[d - 1], first_recv.at[d - 1],
                          *along_first(q))
            copy.start()
            first.append(copy)
    summed = summed.astype(F32)
    for d, copy in enumerate(first):
        copy.wait()
        summed = summed + first_in[d].astype(F32)
    own[...] = summed.astype(BF16)

    second = []
    for d in steps:
        copy = remote(own, second_in.at[there], second_send.at[d - 1], second_recv.at[d - 1],
                      *along_second((there + d) % count))
        copy.start()
        second.append(copy)
    second_in[there] = own[...]
    for copy in second:
        copy.wait()
    summed = second_in[0].astype(F32)
    for q in steps:
        summed = summed + second_in[q].astype(F32)
    place = piece_at(core, here)
    packed_ref[place, :] = summed.astype(BF16)

    give = []

    def pass_on(slot, q):
        at = packed_ref.at[piece_at(core, q), :]
        copy = remote(at, at, give_send.at[slot], give_recv.at[slot], *pair)
        copy.start()
        give.append(copy)

    spread = []
    for d in steps:
        at = packed_ref.at[place, :]
        copy = remote(at, at, spread_send.at[d - 1], spread_recv.at[d - 1], *along_first((here + d) % count))
        copy.start()
        spread.append(copy)
    pass_on(0, here)
    for d in steps:
        spread[d - 1].wait_recv()
        pass_on(d, (here - d + count) % count)
    for copy in spread:
        copy.wait_send()
    for copy in give:
        copy.wait()


def front(orbitals, block_vectors, kernel, count, groups):
    rows, coeffs = orbitals.shape
    block_rows = block_vectors.shape[0]
    bands, vectors, cols = rows * count, block_rows * count, coeffs // count
    _, _, used = blocks_of(bands, vectors)
    pieces = CORES * count
    piece = pl.cdiv(pl.cdiv(used, pieces), 16) * 16
    sems = pltpu.SemaphoreType.DMA
    seven = sems((count - 1,))
    return pl.pallas_call(
        functools.partial(front_kernel, count, groups, coeffs * groups),
        out_shape=(
            jax.ShapeDtypeStruct((pieces * piece, LANES), BF16),
            jax.ShapeDtypeStruct((bands, cols), BF16),
        ),
        in_specs=[VMEM, VMEM, VMEM],
        out_specs=(VMEM, VMEM),
        scratch_shapes=[
            pltpu.VMEM((bands, cols), BF16),
            pltpu.VMEM((vectors, cols), BF16),
            pltpu.VMEM((pieces * piece, LANES), BF16),
            pltpu.VMEM((count * piece, LANES), BF16),
            pltpu.VMEM((count - 1, piece, LANES), BF16),
            pltpu.VMEM((count - 1, piece, LANES), BF16),
            pltpu.VMEM((piece, LANES), BF16),
            pltpu.VMEM((count, piece, LANES), BF16),
            seven, seven, seven, seven, sems, sems,
            seven, seven, seven, seven, seven, seven, sems((count,)), sems((count,)),
        ],
        compiler_params=pltpu.CompilerParams(
            collective_id=0, has_side_effects=True, vmem_limit_bytes=40 * 2**20
        ),
        name="front",
    )(orbitals, block_vectors, kernel[None, :])


def back_kernel(
    count, ace_ref, exchange_ref, ace_out, exchange_out, to_ace, from_ace, to_block, from_block
):
    band, ga = lax.axis_index("band"), lax.axis_index("ga")
    rows, cols = ace_out.shape[0], ace_ref.shape[1]
    block_rows = exchange_out.shape[0]
    steps = range(1, count)
    meet([((band + d) % count, ga) for d in steps])
    place = aligned(band * cols, LANES, cols)
    copies = []
    for d in steps:
        peer = (band + d) % count
        copies.append(
            remote(ace_ref.at[aligned(peer * rows, 16, rows), :], ace_out.at[:, place],
                   to_ace.at[d - 1], from_ace.at[d - 1], peer, ga)
        )
        copies.append(
            remote(exchange_ref.at[aligned(peer * block_rows, 16, block_rows), :], exchange_out.at[:, place],
                   to_block.at[d - 1], from_block.at[d - 1], peer, ga)
        )
    for copy in copies:
        copy.start()
    ace_out[:, place] = ace_ref[aligned(band * rows, 16, rows), :]
    exchange_out[:, place] = exchange_ref[aligned(band * block_rows, 16, block_rows), :]
    for copy in copies:
        copy.wait()


def back(ace, exchange, count):
    bands, cols = ace.shape
    vectors = exchange.shape[0]
    seven = pltpu.SemaphoreType.DMA((count - 1,))
    return pl.pallas_call(
        functools.partial(back_kernel, count),
        out_shape=(
            jax.ShapeDtypeStruct((bands // count, cols * count), BF16),
            jax.ShapeDtypeStruct((vectors // count, cols * count), BF16),
        ),
        in_specs=[VMEM, VMEM],
        out_specs=(VMEM, VMEM),
        scratch_shapes=[seven, seven, seven, seven],
        compiler_params=pltpu.CompilerParams(
            collective_id=1, has_side_effects=True, vmem_limit_bytes=20 * 2**20
        ),
        name="back",
    )(ace, exchange)


def shards(count, groups, orbitals, kernel, block_vectors):
    packed, weighted = front(orbitals, block_vectors, kernel, count, groups)
    ace, exchange = solve(packed, weighted, orbitals.shape[0] * count, block_vectors.shape[0] * count)
    return back(ace, exchange, count)


def solution(mesh):
    placed = (P(("img", "band"), "ga"), P("ga"), P(("img", "band"), "ga"))
    return jax.shard_map(
        functools.partial(shards, mesh.shape["band"], mesh.shape["ga"]),
        mesh=mesh,
        in_specs=placed,
        out_specs=(P(("img", "band"), "ga"), P(("img", "band"), "ga")),
        check_vma=False,
    )
```

time: 515 us -> 133 us (0.26)
  other arithmetic: 193 us -> 0 us
  waiting for transfers between devices: 159 us -> 0 us
  Pallas kernels: 0 us -> 128 us
  blocking collectives: 70.3 us -> 0 us
  matrix products: 37 us -> 0 us
  local copies, waits for them, and re-layouts: 26.8 us -> 4.18 us
  between operations: 18.2 us -> 0.67 us
  starting transfers between devices: 6.6 us -> 0 us
    another operation x25 -> x0, other arithmetic: 185 us -> none  [the longest x22 124 us: shards(): factor = jnp.linalg.cholesky(margin)]
    pallas_call x0 -> x3, Pallas kernels: none -> 128 us  [the longest x1 70.9 us: front(): pl.pallas_call(functools.partial(front_kernel, count, groups, coeffs * gr...]
    all_gather x3 -> x0, waiting for transfers between devices: 122 us -> none  [the longest x1 80.9 us: shards(): lax.all_gather(orbitals, 'band', axis=0, tiled=True)]
    all_to_all x2 -> x0, blocking collectives: 70.3 us -> none  [the longest x1 43 us: sent_and_summed(): lax.all_to_all(pieces, axis, split_axis=0, concat_axis=0, tiled=True)]
    all_to_all x1 -> x0, waiting for transfers between devices: 35.2 us -> none  [from_everyone(): lax.all_to_all(jnp.broadcast_to(shard[None], (count, *shard.shape)), axis...]
    another operation x21 -> x0, matrix products: 22.9 us -> none  [the longest x11 13.1 us: shards(): lax.linalg.triangular_solve(factor, identity, left_side=True, lower=True)]
    another operation x25 -> x0, local copies, waits for them, and re-layouts: 21.7 us -> none
    dot_general x4 -> x0, matrix products: 14.2 us -> none  [the longest x1 4.75 us: shards(): lax.dot_general(orbitals, weighted, (((1,), (1,)), ((), ())), preferred_e...]
  transfers between devices with their start and end apart: 4 -> 0, of which waited for: 3 -> 0; matrix products, arithmetic and copies ran while one was open for 47% -> 0% of each run, Pallas kernels for 0% -> 0%
where the time goes in v1:
time: 133 us
  Pallas kernels  128 us (96%)
  local copies, waits for them, and re-layouts  4.18 us (3%)
    pallas_call x1, Pallas kernels, front(): pl.pallas_call(functools.partial(front_kernel, count, groups, coeffs * gr...  70.9 us
    pallas_call x1, Pallas kernels, solve(): pl.pallas_call(functools.partial(solve_kernel, bands, vectors), out_shape...  34.2 us
    pallas_call x1, Pallas kernels, back(): pl.pallas_call(functools.partial(back_kernel, count), out_shape=(jax.Shap...  22.7 us
    unnamed x8, local copies, waits for them, and re-layouts  4.18 us

profile of v1, /device:TPU:513, one launch (start us, length us, event | category | flops | bytes accessed | tf_op | source)
XLA Modules:
  0.0 132.6 jit_solution(9314651188244579306)
XLA Ops:
  0.6 0.0 copy-start
  0.6 1.1 copy-done
  1.7 0.0 copy-start.1
  1.7 0.9 copy-done.1
  2.6 0.0 copy-start.2
  2.6 0.7 copy-done.2
  3.3 70.9 %front.1 = (bf16[4352,128]{1,0:T(8,128)(2,1)S(1)}, bf16[768,384]{1,0:T(8,128)(2,1)S(1)}) custom-call(bf16[96,3072]{1,0:T(8,128)(2,1)S(1)} %copy-done, bf16[32,3072]{1,0:T(8,128)(2,1)S(1)} %copy-done.1, f32[1,3072]{1,0:T(1,128)S(1)} %bitcast.1), custom_call_target="tpu_custom_call" | custom-call | tf_op jit(solution)/shard_map/front/pallas_call | solution.py:315
  74.2 34.2 %solve.1 = (bf16[768,384]{1,0:T(8,128)(2,1)S(1)}, bf16[256,384]{1,0:T(8,128)(2,1)S(1)}) custom-call(bf16[4352,128]{1,0:T(8,128)(2,1)S(1)} %get-tuple-element.6.packed_ref, bf16[768,384]{1,0:T(8,128)(2,1)S(1)} %get-tuple-element.7.weighted_ref), custom_call_target="tpu_custom_call" | custom-call | tf_op jit(solution)/shard_map/solve/pallas_call | solution.py:133
  108.4 22.7 %back.1 = (bf16[96,3072]{1,0:T(8,128)(2,1)S(1)}, bf16[32,3072]{1,0:T(8,128)(2,1)S(1)}) custom-call(bf16[768,384]{1,0:T(8,128)(2,1)S(1)} %get-tuple-element.8.ace_ref, bf16[256,384]{1,0:T(8,128)(2,1)S(1)} %get-tuple-element.9.exchange_ref), custom_call_target="tpu_custom_call" | custom-call | tf_op jit(solution)/shard_map/back/pallas_call | solution.py:374
  131.1 0.8 copy.7
  131.9 0.7 copy.8
Async XLA Ops:
  0.6 1.1 copy-start
  1.7 0.9 copy-start.1
  2.6 0.7 copy-start.2

commit v2 on v0

v2 whole, which is shorter than its diff:
```python
import functools
import jax
import jax.numpy as jnp
from jax import lax
from jax.experimental import pallas as pl
from jax.experimental.pallas import tpu as pltpu
from jax.sharding import PartitionSpec as P

LANES = 128
SUB = 8
TILE = 128
PANEL = 32
GROUP = 2
CORES = 2
MESH = pl.DeviceIdType.MESH
F32 = jnp.float32
BF16 = jnp.bfloat16
VMEM = pl.BlockSpec(memory_space=pltpu.VMEM)


def row_of(value, index):
    return jnp.broadcast_to(value[index : index + 1, :], value.shape)


def column_of(value, index):
    return jnp.take_along_axis(value, jnp.full(value.shape, index, jnp.int32), axis=1)


def inverse_factor(rows):
    sub = lax.broadcasted_iota(jnp.int32, (SUB, LANES), 0)
    lane = lax.broadcasted_iota(jnp.int32, (SUB, LANES), 1)
    rows = list(rows)
    count = len(rows)
    per_panel = PANEL // SUB
    size = GROUP * SUB
    done = []
    for begin in range(0, count, GROUP):
        first = begin * SUB
        last = (begin // per_panel + 1) * per_panel
        inside = (lane >= first) & (lane < first + size)
        strips = rows[begin : begin + GROUP]
        columns = [[column_of(strip, first + k) for k in range(size)] for strip in strips]
        solved = [
            jnp.where(inside, jnp.where(lane - first == sub + s * SUB, 1.0, 0.0), strips[s])
            for s in range(GROUP)
        ]
        forward = list(solved)
        scale = [jnp.ones((SUB, LANES), F32)] * GROUP
        diagonal = [jnp.ones((SUB, LANES), F32)] * GROUP
        for j in range(size):
            js, jj = divmod(j, SUB)
            value = row_of(columns[js][j], jj)
            pivot = 1.0 / value
            here = sub == jj
            scale[js] = jnp.where(here, pivot, scale[js])
            diagonal[js] = jnp.where(here, value, diagonal[js])
            factor = [columns[s][j] * pivot for s in range(GROUP)]
            factor[js] = jnp.where(here, 0.0, factor[js])
            for k in range(j + 1, size):
                row = row_of(columns[js][k], jj)
                for s in range(GROUP):
                    columns[s][k] = columns[s][k] - factor[s] * row
            row = row_of(forward[js], jj)
            if jj < SUB - 1:
                forward[js] = forward[js] - jnp.where(sub > jj, factor[js], 0.0) * row
            for s in range(js + 1, GROUP):
                forward[s] = forward[s] - factor[s] * row
            row = row_of(solved[js], jj)
            for s in range(GROUP):
                solved[s] = solved[s] - factor[s] * row
        for s in range(GROUP):
            kept = forward[s] * lax.rsqrt(diagonal[s])
            stop = first + (s + 1) * SUB
            if stop < last * SUB:
                kept = jnp.where((lane < stop) | (lane >= last * SUB), kept, 0.0)
            done.append(kept)
        after = begin + GROUP
        if after < last:
            solved_rows = [row_of(solved[s] * scale[s], jj) for s in range(GROUP) for jj in range(SUB)]
            for r in range(after, last):
                old = rows[r]
                total = jnp.where(inside, 0.0, old)
                terms = [column_of(old, first + j) * solved_rows[j] for j in range(size)]
                while len(terms) > 1:
                    terms = [terms[i] + terms[i + 1] for i in range(0, len(terms), 2)]
                rows[r] = total - terms[0]
        elif last < count:
            start = last - per_panel
            upper = jnp.concatenate(done[start:last], axis=0)
            product = dot_split(split(upper.T), split(upper))
            gone = (lane >= start * SUB) & (lane < last * SUB)
            for r in range(last, count):
                rows[r] = jnp.where(gone, 0.0, rows[r]) - product[r * SUB : r * SUB + SUB, :]
    return [jnp.where(lane < (t + 1) * SUB, done[t], 0.0) for t in range(count)]


def split(value):
    high = value.astype(BF16)
    return high, (value - high.astype(F32)).astype(BF16)


def dot(left, right):
    return lax.dot_general(left, right, (((1,), (0,)), ((), ())), preferred_element_type=F32)


def dot_rows(left, right):
    return lax.dot_general(left, right, (((1,), (1,)), ((), ())), preferred_element_type=F32)


def dot_split(left, right):
    (lh, ll), (rh, rl) = left, right
    return dot(lh, rh) + dot(lh, rl) + dot(ll, rh)


def remote(src, dst, send, recv, band, ga):
    return pltpu.make_async_remote_copy(
        src_ref=src,
        dst_ref=dst,
        send_sem=send,
        recv_sem=recv,
        device_id={"band": band, "ga": ga},
        device_id_type=MESH,
    )


def meet(devices):
    barrier = pltpu.get_barrier_semaphore()
    for band, ga in devices:
        pl.semaphore_signal(barrier, inc=1, device_id={"band": band, "ga": ga}, device_id_type=MESH)
    pl.semaphore_wait(barrier, len(devices))


def aligned(start, step, size):
    return pl.ds(pl.multiple_of(start, step), size)


def ring(position, count):
    return [(position + d) % count for d in range(1, count)]


def all_reduce(count, place, part, half_in, half, first_in, own, second_in, out, send, recv):
    core, here, there, along_first, along_second, pair = place
    piece = part.shape[0] // (CORES * count)
    size = piece * count
    pair_at, first_at, second_at, spread_at, give_at = 0, 1, count, 2 * count - 1, 3 * count - 2
    steps = range(1, count)

    def piece_at(q):
        return aligned((core * count + q) * piece, 16, piece)

    def copy_to(src, dst, sem, device):
        copy = remote(src, dst, send.at[sem], recv.at[sem], *device)
        copy.start()
        return copy

    swap = copy_to(part.at[aligned((1 - core) * size, 16, size), :], half_in, pair_at, pair)
    yield
    swap.wait()
    copies = []
    for d in range(1, count + 1):
        q = (here + d) % count
        theirs = half_in[aligned(q * piece, 16, piece), :].astype(F32)
        summed = part[piece_at(q), :].astype(F32) + theirs
        if d < count:
            half[d - 1] = summed.astype(BF16)
            copies.append(copy_to(half.at[d - 1], first_in.at[d - 1], first_at + d - 1, along_first(q)))
    yield
    for d, copy in enumerate(copies):
        copy.wait()
        summed = summed + first_in[d].astype(F32)
    own[...] = summed.astype(BF16)
    copies = []
    for d in steps:
        device = along_second((there + d) % count)
        copies.append(copy_to(own, second_in.at[there], second_at + d - 1, device))
    second_in[there] = own[...]
    yield
    for copy in copies:
        copy.wait()
    summed = second_in[0].astype(F32)
    for q in steps:
        summed = summed + second_in[q].astype(F32)
    out[piece_at(here), :] = summed.astype(BF16)
    copies, given = [], []

    def pass_on(slot, q):
        at = out.at[piece_at(q), :]
        given.append(copy_to(at, at, give_at + slot, pair))

    for d in steps:
        at = out.at[piece_at(here), :]
        copies.append(copy_to(at, at, spread_at + d - 1, along_first((here + d) % count)))
    pass_on(0, here)
    yield
    for d in steps:
        copies[d - 1].wait_recv()
        pass_on(d, (here - d + count) % count)
    yield
    for copy in copies:
        copy.wait_send()
    for copy in given:
        copy.wait()
    yield


def ace_kernel(
    count, groups, orbitals_ref, block_ref, kernel_ref, ace_out, exchange_out,
    orbitals, block, gains, bands, vectors, weighted, work, ace, exchange,
    margin_part, margin_half_in, margin_half, margin_first, margin_own, margin_second, margin,
    overlap_part, overlap_half_in, overlap_half, overlap_first, overlap_own, overlap_second, overlap,
    load, to_bands, from_bands, to_vectors, from_vectors, margin_send, margin_recv, overlap_send, overlap_recv,
    to_ace, from_ace, to_block, from_block,
):
    band, ga = lax.axis_index("band"), lax.axis_index("ga")
    line, core = ga // CORES, ga % CORES
    rows, cols = orbitals.shape[0], weighted.shape[1]
    block_rows = block.shape[0]
    total = orbitals.shape[1] * groups
    here = (1 - core) * band + core * line
    there = (1 - core) * line + core * band

    def along_first(q):
        return (1 - core) * q + core * band, CORES * ((1 - core) * line + core * q) + core

    def along_second(q):
        return (1 - core) * band + core * q, CORES * ((1 - core) * q + core * line) + core

    pair = (band, CORES * line + 1 - core)
    place = (core, here, there, along_first, along_second, pair)

    loads = [
        pltpu.make_async_copy(orbitals_ref, orbitals, load.at[0]),
        pltpu.make_async_copy(block_ref, block, load.at[1]),
        pltpu.make_async_copy(kernel_ref, gains, load.at[2]),
    ]
    for copy in loads:
        copy.start()
    meet(
        [along_first(q) for q in ring(here, count)]
        + [along_second(q) for q in ring(there, count)]
        + [pair]
    )
    for copy in loads:
        copy.wait()

    mine = aligned(band * cols, LANES, cols)
    band_rows = aligned(band * rows, 16, rows)
    vector_rows = aligned(band * block_rows, 16, block_rows)
    moved, moved_block = [], []
    for d, peer in enumerate(ring(band, count)):
        theirs = aligned(peer * cols, LANES, cols)
        moved.append(
            remote(orbitals.at[:, theirs], bands.at[band_rows, :], to_bands.at[d], from_bands.at[d], peer, ga)
        )
        moved_block.append(
            remote(block.at[:, theirs], vectors.at[vector_rows, :], to_vectors.at[d], from_vectors.at[d], peer, ga)
        )
    for copy in moved + moved_block:
        copy.start()
    bands[band_rows, :] = orbitals[:, mine]
    vectors[vector_rows, :] = block[:, mine]
    gain = gains[:, mine]
    for copy in moved:
        copy.wait()

    all_rows, all_vectors = bands.shape[0], vectors.shape[0]
    tiles, vector_tiles = all_rows // TILE, all_vectors // TILE
    corner = [(i, j) for i in range(tiles) for j in range(i, tiles)]
    corner = {ij: n * TILE for n, ij in enumerate(corner)}
    flat = {(i, j): (i * vector_tiles + j) * TILE for i in range(tiles) for j in range(vector_tiles)}
    for i in range(tiles):
        at = pl.ds(i * TILE, TILE)
        weighted[at, :] = (-(bands[at, :].astype(F32) * gain)).astype(BF16)
    for i in range(tiles):
        at, after = pl.ds(i * TILE, TILE), pl.ds(i * TILE, all_rows - i * TILE)
        sums = dot_rows(bands[at, :], weighted[after, :]) + dot_rows(weighted[at, :], bands[after, :])
        sums = (sums * (-0.5 / total)).astype(BF16)
        for j in range(i, tiles):
            margin_part[pl.ds(corner[i, j], TILE), :] = sums[:, (j - i) * TILE : (j - i + 1) * TILE]
    used = len(corner) * TILE
    if used < margin_part.shape[0]:
        margin_part[used:, :] = jnp.zeros((margin_part.shape[0] - used, LANES), BF16)
    margin_steps = all_reduce(
        count, place, margin_part, margin_half_in, margin_half, margin_first, margin_own, margin_second, margin,
        margin_send, margin_recv,
    )
    next(margin_steps)

    for copy in moved_block:
        copy.wait()
    for i in range(tiles):
        sums = dot_rows(weighted[pl.ds(i * TILE, TILE), :], vectors[...])
        sums = (sums * (1.0 / total)).astype(BF16)
        for j in range(vector_tiles):
            overlap_part[pl.ds(flat[i, j], TILE), :] = sums[:, j * TILE : (j + 1) * TILE]
    used = len(flat) * TILE
    if used < overlap_part.shape[0]:
        overlap_part[used:, :] = jnp.zeros((overlap_part.shape[0] - used, LANES), BF16)
    overlap_steps = all_reduce(
        count, place, overlap_part, overlap_half_in, overlap_half, overlap_first, overlap_own, overlap_second,
        overlap, overlap_send, overlap_recv,
    )
    next(overlap_steps)
    for _ in range(3):
        next(margin_steps)
        next(overlap_steps)
    for i in range(tiles):
        at = pl.ds(i * TILE, TILE)
        work[at, pl.ds(all_rows, cols)] = weighted[at, :].astype(F32)
    next(margin_steps)
    next(margin_steps)

    for (i, j), row in corner.items():
        work[pl.ds(i * TILE, TILE), pl.ds(j * TILE, TILE)] = margin[pl.ds(row, TILE), :].astype(F32)
    edge = all_rows + cols
    segments, applied, early = [], None, None
    for k in range(tiles):
        top = k * TILE
        strips = [work[pl.ds(top + SUB * t, SUB), pl.ds(top, TILE)] for t in range(TILE // SUB)]
        inverse = split(jnp.concatenate(inverse_factor(strips), axis=0))
        first = top + TILE
        if k == 0:
            next(overlap_steps)
        if k == 1:
            next(overlap_steps)
            for (i, j), row in flat.items():
                work[pl.ds(i * TILE, TILE), pl.ds(edge + j * TILE, TILE)] = overlap[pl.ds(row, TILE), :].astype(F32)
            early_inverse, early_lower, early_projector = early
            coupling = dot_split(early_inverse, split(work[pl.ds(0, TILE), pl.ds(edge, all_vectors)]))
            coupling_parts = split(coupling)
            for i in range(1, tiles):
                at = pl.ds(i * TILE, TILE), pl.ds(edge, all_vectors)
                work[at] = work[at] - dot_split(early_lower[i - 1], coupling_parts)
            applied = dot_split(split(coupling.T), early_projector)
        stop = edge if k == 0 else edge + all_vectors
        upper = dot_split(inverse, split(work[pl.ds(top, TILE), pl.ds(first, stop - first)]))
        parts = split(upper)
        lowers = [split(upper[:, i * TILE - first : (i + 1) * TILE - first].T) for i in range(k + 1, tiles)]
        for i in range(k + 1, tiles):
            cut = tuple(part[:, i * TILE - first :] for part in parts)
            at = pl.ds(i * TILE, TILE), pl.ds(i * TILE, stop - i * TILE)
            work[at] = work[at] - dot_split(lowers[i - k - 1], cut)
        base = all_rows - first
        projector = tuple(part[:, base : base + cols] for part in parts)
        ace[pl.ds(top, TILE), :] = projector[0]
        for p in range(count):
            low, high = max(top, p * rows), min(first, (p + 1) * rows)
            if low < high:
                target = pl.ds(low - p * rows, high - low)
                copy = remote(
                    ace.at[pl.ds(low, high - low), :], ace_out.at[target, mine],
                    to_ace.at[len(segments)], from_ace.at[band], p, ga,
                )
                segments.append((p, copy))
                pl.when(band != p)(copy.start)

                @pl.when(band == p)
                def _(low=low, high=high, target=target):
                    ace_out[target, mine] = ace[pl.ds(low, high - low), :]

        if k == 0:
            early = inverse, lowers, projector
        else:
            coupling = split(upper[:, base + cols :].T)
            applied = applied + dot_split(coupling, projector)
    exchange[...] = (-applied).astype(BF16)

    blocks = []
    for d, peer in enumerate(ring(band, count)):
        copy = remote(
            exchange.at[aligned(peer * block_rows, 16, block_rows), :], exchange_out.at[:, mine],
            to_block.at[d], from_block.at[d], peer, ga,
        )
        copy.start()
        blocks.append(copy)
    exchange_out[:, mine] = exchange[vector_rows, :]
    for p, copy in segments:
        pl.when(band != p)(copy.wait_send)
    for q in ring(band, count):
        remote(
            ace.at[pl.ds(0, rows), :], ace_out.at[:, aligned(q * cols, LANES, cols)],
            to_ace.at[0], from_ace.at[q], q, ga,
        ).wait_recv()
    for copy in blocks:
        copy.wait()


def ace_of(count, groups, orbitals, kernel, block_vectors):
    rows, coeffs = orbitals.shape
    block_rows = block_vectors.shape[0]
    bands, vectors, cols = rows * count, block_rows * count, coeffs // count
    tiles = bands // TILE
    dma = pltpu.SemaphoreType.DMA

    def reduced(used):
        pieces = CORES * count
        piece = pl.cdiv(pl.cdiv(used, pieces), 16) * 16
        return [
            pltpu.VMEM((pieces * piece, LANES), BF16),
            pltpu.VMEM((count * piece, LANES), BF16),
            pltpu.VMEM((count - 1, piece, LANES), BF16),
            pltpu.VMEM((count - 1, piece, LANES), BF16),
            pltpu.VMEM((piece, LANES), BF16),
            pltpu.VMEM((count, piece, LANES), BF16),
            pltpu.VMEM((pieces * piece, LANES), BF16),
        ]

    others = dma((count - 1,))
    reducing = dma((4 * count - 2,))
    anywhere = pl.BlockSpec(memory_space=pl.ANY)
    return pl.pallas_call(
        functools.partial(ace_kernel, count, groups),
        out_shape=(
            jax.ShapeDtypeStruct((rows, coeffs), BF16),
            jax.ShapeDtypeStruct((block_rows, coeffs), BF16),
        ),
        in_specs=[anywhere, anywhere, anywhere],
        out_specs=(VMEM, VMEM),
        scratch_shapes=[
            pltpu.VMEM((rows, coeffs), BF16),
            pltpu.VMEM((block_rows, coeffs), BF16),
            pltpu.VMEM((1, coeffs), F32),
            pltpu.VMEM((bands, cols), BF16),
            pltpu.VMEM((vectors, cols), BF16),
            pltpu.VMEM((bands, cols), BF16),
            pltpu.VMEM((bands, bands + cols + vectors), F32),
            pltpu.VMEM((bands, cols), BF16),
            pltpu.VMEM((vectors, cols), BF16),
            *reduced(tiles * (tiles + 1) // 2 * TILE),
            *reduced(tiles * (vectors // TILE) * TILE),
            dma((3,)), others, others, others, others, reducing, reducing, reducing, reducing,
            dma((tiles + count,)), dma((count,)), others, others,
        ],
        compiler_params=pltpu.CompilerParams(
            collective_id=0, has_side_effects=True, vmem_limit_bytes=48 * 2**20
        ),
        name="ace",
    )(orbitals, block_vectors, kernel[None, :])


def solution(mesh):
    placed = (P(("img", "band"), "ga"), P("ga"), P(("img", "band"), "ga"))
    return jax.shard_map(
        functools.partial(ace_of, mesh.shape["band"], mesh.shape["ga"]),
        mesh=mesh,
        in_specs=placed,
        out_specs=(P(("img", "band"), "ga"), P(("img", "band"), "ga")),
        check_vma=False,
    )
```

time: 515 us -> 112 us (0.22)
  other arithmetic: 193 us -> 0 us
  waiting for transfers between devices: 159 us -> 0 us
  Pallas kernels: 0 us -> 107 us
  blocking collectives: 70.3 us -> 0 us
  matrix products: 37 us -> 0 us
  local copies, waits for them, and re-layouts: 26.8 us -> 4.18 us
  between operations: 18.2 us -> 0.65 us
  starting transfers between devices: 6.6 us -> 0 us
    another operation x25 -> x0, other arithmetic: 185 us -> none  [the longest x22 124 us: shards(): factor = jnp.linalg.cholesky(margin)]
    all_gather x3 -> x0, waiting for transfers between devices: 122 us -> none  [the longest x1 80.9 us: shards(): lax.all_gather(orbitals, 'band', axis=0, tiled=True)]
    pallas_call x0 -> x1, Pallas kernels: none -> 107 us  [ace_of(): pl.pallas_call(functools.partial(ace_kernel, count, groups), out_shape=(j...]
    all_to_all x2 -> x0, blocking collectives: 70.3 us -> none  [the longest x1 43 us: sent_and_summed(): lax.all_to_all(pieces, axis, split_axis=0, concat_axis=0, tiled=True)]
    all_to_all x1 -> x0, waiting for transfers between devices: 35.2 us -> none  [from_everyone(): lax.all_to_all(jnp.broadcast_to(shard[None], (count, *shard.shape)), axis...]
    another operation x21 -> x0, matrix products: 22.9 us -> none  [the longest x11 13.1 us: shards(): lax.linalg.triangular_solve(factor, identity, left_side=True, lower=True)]
    another operation x25 -> x0, local copies, waits for them, and re-layouts: 21.7 us -> none
    dot_general x4 -> x0, matrix products: 14.2 us -> none  [the longest x1 4.75 us: shards(): lax.dot_general(orbitals, weighted, (((1,), (1,)), ((), ())), preferred_e...]
  transfers between devices with their start and end apart: 4 -> 0, of which waited for: 3 -> 0; matrix products, arithmetic and copies ran while one was open for 47% -> 0% of each run, Pallas kernels for 0% -> 0%
where the time goes in v2:
time: 112 us
  Pallas kernels  107 us (96%)
  local copies, waits for them, and re-layouts  4.18 us (4%)
    pallas_call x1, Pallas kernels, ace_of(): pl.pallas_call(functools.partial(ace_kernel, count, groups), out_shape=(j...  107 us
    unnamed x8, local copies, waits for them, and re-layouts  4.18 us

profile of v2, /device:TPU:513, one launch (start us, length us, event | category | flops | bytes accessed | tf_op | source)
XLA Modules:
  0.0 111.6 jit_solution(5923523218811903086)
XLA Ops:
  0.6 0.0 copy-start
  0.6 1.1 copy-done
  1.7 0.0 copy-start.1
  1.7 0.9 copy-done.1
  2.6 0.0 copy-start.2
  2.6 0.7 copy-done.2
  3.3 106.8 %ace.1 = (bf16[96,3072]{1,0:T(8,128)(2,1)S(1)}, bf16[32,3072]{1,0:T(8,128)(2,1)S(1)}) custom-call(bf16[96,3072]{1,0:T(8,128)(2,1)S(1)} %copy-done, bf16[32,3072]{1,0:T(8,128)(2,1)S(1)} %copy-done.1, f32[1,3072]{1,0:T(1,128)S(1)} %bitcast.1), custom_call_target="tpu_custom_call" | custom-call | tf_op jit(solution)/shard_map/ace/pallas_call | solution.py:411
  110.1 0.8 copy.7
  110.9 0.7 copy.8
Async XLA Ops:
  0.6 1.1 copy-start
  1.7 0.9 copy-start.1
  2.6 0.7 copy-start.2

commit v3 on v2

--- a/solution.py
+++ b/solution.py
@@ -26,7 +26,7 @@
     return jnp.take_along_axis(value, jnp.full(value.shape, index, jnp.int32), axis=1)
 
 
-def inverse_factor(rows):
+def inverse_factor(rows, between=None):
     sub = lax.broadcasted_iota(jnp.int32, (SUB, LANES), 0)
     lane = lax.broadcasted_iota(jnp.int32, (SUB, LANES), 1)
     rows = list(rows)
@@ -85,6 +85,8 @@
                     terms = [terms[i] + terms[i + 1] for i in range(0, len(terms), 2)]
                 rows[r] = total - terms[0]
         elif last < count:
+            if between is not None and last == count - per_panel:
+                between()
             start = last - per_panel
             upper = jnp.concatenate(done[start:last], axis=0)
             product = dot_split(split(upper.T), split(upper))
@@ -206,11 +208,11 @@
 def ace_kernel(
     count, groups, orbitals_ref, block_ref, kernel_ref, ace_out, exchange_out,
     orbitals, block, gains, bands, vectors, weighted, work, ace, exchange,
-    margin_part, margin_half_in, margin_half, margin_first, margin_own, margin_second, margin,
-    overlap_part, overlap_half_in, overlap_half, overlap_first, overlap_own, overlap_second, overlap,
-    load, to_bands, from_bands, to_vectors, from_vectors, margin_send, margin_recv, overlap_send, overlap_recv,
-    to_ace, from_ace, to_block, from_block,
+    *rest,
 ):
+    head_refs, tail_refs, overlap_refs = rest[:7], rest[7:14], rest[14:21]
+    (load, to_bands, from_bands, to_vectors, from_vectors, head_send, head_recv, tail_send, tail_recv,
+     overlap_send, overlap_recv, to_ace, from_ace, to_block, from_block) = rest[21:]
     band, ga = lax.axis_index("band"), lax.axis_index("ga")
     line, core = ga // CORES, ga % CORES
     rows, cols = orbitals.shape[0], weighted.shape[1]
@@ -265,84 +267,113 @@
 
     all_rows, all_vectors = bands.shape[0], vectors.shape[0]
     tiles, vector_tiles = all_rows // TILE, all_vectors // TILE
-    corner = [(i, j) for i in range(tiles) for j in range(i, tiles)]
-    corner = {ij: n * TILE for n, ij in enumerate(corner)}
+    head = {(0, j): j * TILE for j in range(tiles)}
+    tail = [(i, j) for i in range(1, tiles) for j in range(i, tiles)]
+    tail = {ij: n * TILE for n, ij in enumerate(tail)}
     flat = {(i, j): (i * vector_tiles + j) * TILE for i in range(tiles) for j in range(vector_tiles)}
-    for i in range(tiles):
-        at = pl.ds(i * TILE, TILE)
-        weighted[at, :] = (-(bands[at, :].astype(F32) * gain)).astype(BF16)
-    for i in range(tiles):
+
+    def clear_after(where, part):
+        used = len(where) * TILE
+        if used < part.shape[0]:
+            part[used:, :] = jnp.zeros((part.shape[0] - used, LANES), BF16)
+
+    def margin_rows(i, where, part):
         at, after = pl.ds(i * TILE, TILE), pl.ds(i * TILE, all_rows - i * TILE)
         sums = dot_rows(bands[at, :], weighted[after, :]) + dot_rows(weighted[at, :], bands[after, :])
         sums = (sums * (-0.5 / total)).astype(BF16)
         for j in range(i, tiles):
-            margin_part[pl.ds(corner[i, j], TILE), :] = sums[:, (j - i) * TILE : (j - i + 1) * TILE]
-    used = len(corner) * TILE
-    if used < margin_part.shape[0]:
-        margin_part[used:, :] = jnp.zeros((margin_part.shape[0] - used, LANES), BF16)
-    margin_steps = all_reduce(
-        count, place, margin_part, margin_half_in, margin_half, margin_first, margin_own, margin_second, margin,
-        margin_send, margin_recv,
-    )
-    next(margin_steps)
-
+            part[pl.ds(where[i, j], TILE), :] = sums[:, (j - i) * TILE : (j - i + 1) * TILE]
+
+    for i in range(tiles):
+        at = pl.ds(i * TILE, TILE)
+        weighted[at, :] = (-(bands[at, :].astype(F32) * gain)).astype(BF16)
+    margin_rows(0, head, head_refs[0])
+    clear_after(head, head_refs[0])
+    head_steps = all_reduce(count, place, *head_refs, head_send, head_recv)
+    next(head_steps)
+    for i in range(1, tiles):
+        margin_rows(i, tail, tail_refs[0])
+    clear_after(tail, tail_refs[0])
+    tail_steps = all_reduce(count, place, *tail_refs, tail_send, tail_recv)
+    next(tail_steps)
+    next(head_steps)
     for copy in moved_block:
         copy.wait()
     for i in range(tiles):
         sums = dot_rows(weighted[pl.ds(i * TILE, TILE), :], vectors[...])
         sums = (sums * (1.0 / total)).astype(BF16)
         for j in range(vector_tiles):
-            overlap_part[pl.ds(flat[i, j], TILE), :] = sums[:, j * TILE : (j + 1) * TILE]
-    used = len(flat) * TILE
-    if used < overlap_part.shape[0]:
-        overlap_part[used:, :] = jnp.zeros((overlap_part.shape[0] - used, LANES), BF16)
-    overlap_steps = all_reduce(
-        count, place, overlap_part, overlap_half_in, overlap_half, overlap_first, overlap_own, overlap_second,
-        overlap, overlap_send, overlap_recv,
-    )
+            overlap_refs[0][pl.ds(flat[i, j], TILE), :] = sums[:, j * TILE : (j + 1) * TILE]
+    clear_after(flat, overlap_refs[0])
+    overlap_steps = all_reduce(count, place, *overlap_refs, overlap_send, overlap_recv)
     next(overlap_steps)
-    for _ in range(3):
-        next(margin_steps)
-        next(overlap_steps)
+    next(tail_steps)
+    next(head_steps)
+    next(overlap_steps)
+    next(tail_steps)
+    next(head_steps)
+    next(overlap_steps)
+    next(tail_steps)
     for i in range(tiles):
         at = pl.ds(i * TILE, TILE)
         work[at, pl.ds(all_rows, cols)] = weighted[at, :].astype(F32)
-    next(margin_steps)
-    next(margin_steps)
-
-    for (i, j), row in corner.items():
-        work[pl.ds(i * TILE, TILE), pl.ds(j * TILE, TILE)] = margin[pl.ds(row, TILE), :].astype(F32)
+    next(head_steps)
+    next(overlap_steps)
+    next(head_steps)
+
+    def unpack(where, out, column):
+        for (i, j), row in where.items():
+            work[pl.ds(i * TILE, TILE), pl.ds(column + j * TILE, TILE)] = out[pl.ds(row, TILE), :].astype(F32)
+
+    def factored(value, between=None):
+        strips = [value[SUB * t : SUB * (t + 1), :] for t in range(TILE // SUB)]
+        return split(jnp.concatenate(inverse_factor(strips, between), axis=0))
+
+    unpack(head, head_refs[-1], 0)
+    inverse = factored(work[pl.ds(0, TILE), pl.ds(0, TILE)], lambda: next(tail_steps))
+    next(tail_steps)
+    next(overlap_steps)
+    unpack(tail, tail_refs[-1], 0)
     edge = all_rows + cols
     segments, applied, early = [], None, None
     for k in range(tiles):
         top = k * TILE
-        strips = [work[pl.ds(top + SUB * t, SUB), pl.ds(top, TILE)] for t in range(TILE // SUB)]
-        inverse = split(jnp.concatenate(inverse_factor(strips), axis=0))
         first = top + TILE
-        if k == 0:
-            next(overlap_steps)
+        ours = pl.ds(top, TILE)
         if k == 1:
             next(overlap_steps)
-            for (i, j), row in flat.items():
-                work[pl.ds(i * TILE, TILE), pl.ds(edge + j * TILE, TILE)] = overlap[pl.ds(row, TILE), :].astype(F32)
-            early_inverse, early_lower, early_projector = early
+        ending = k == tiles - 1
+        if not ending:
+            at = pl.ds(first, TILE)
+            ahead = split(dot_split(inverse, split(work[ours, at])))
+            lower = split((ahead[0].astype(F32) + ahead[1].astype(F32)).T)
+            following = factored(work[at, at] - dot_split(lower, ahead))
+            lowers = [lower]
+        else:
+            lowers = []
+        if k == 1:
+            unpack(flat, overlap_refs[-1], edge)
+            early_inverse, early_lowers, early_projector = early
             coupling = dot_split(early_inverse, split(work[pl.ds(0, TILE), pl.ds(edge, all_vectors)]))
             coupling_parts = split(coupling)
             for i in range(1, tiles):
                 at = pl.ds(i * TILE, TILE), pl.ds(edge, all_vectors)
-                work[at] = work[at] - dot_split(early_lower[i - 1], coupling_parts)
+                work[at] = work[at] - dot_split(early_lowers[i - 1], coupling_parts)
             applied = dot_split(split(coupling.T), early_projector)
+        start = min(first + TILE, all_rows)
         stop = edge if k == 0 else edge + all_vectors
-        upper = dot_split(inverse, split(work[pl.ds(top, TILE), pl.ds(first, stop - first)]))
+        upper = dot_split(inverse, split(work[ours, pl.ds(start, stop - start)]))
         parts = split(upper)
-        lowers = [split(upper[:, i * TILE - first : (i + 1) * TILE - first].T) for i in range(k + 1, tiles)]
+        for i in range(k + 2, tiles):
+            lowers.append(split(upper[:, i * TILE - start : (i + 1) * TILE - start].T))
         for i in range(k + 1, tiles):
-            cut = tuple(part[:, i * TILE - first :] for part in parts)
-            at = pl.ds(i * TILE, TILE), pl.ds(i * TILE, stop - i * TILE)
+            low = max(i * TILE, start)
+            cut = tuple(part[:, low - start :] for part in parts)
+            at = pl.ds(i * TILE, TILE), pl.ds(low, stop - low)
             work[at] = work[at] - dot_split(lowers[i - k - 1], cut)
-        base = all_rows - first
+        base = all_rows - start
         projector = tuple(part[:, base : base + cols] for part in parts)
-        ace[pl.ds(top, TILE), :] = projector[0]
+        ace[ours, :] = projector[0]
         for p in range(count):
             low, high = max(top, p * rows), min(first, (p + 1) * rows)
             if low < high:
@@ -363,6 +394,8 @@
         else:
             coupling = split(upper[:, base + cols :].T)
             applied = applied + dot_split(coupling, projector)
+        if not ending:
+            inverse = following
     exchange[...] = (-applied).astype(BF16)
 
     blocks = []
@@ -426,13 +459,15 @@
             pltpu.VMEM((bands, bands + cols + vectors), F32),
             pltpu.VMEM((bands, cols), BF16),
             pltpu.VMEM((vectors, cols), BF16),
-            *reduced(tiles * (tiles + 1) // 2 * TILE),
+            *reduced(tiles * TILE),
+            *reduced(tiles * (tiles - 1) // 2 * TILE),
             *reduced(tiles * (vectors // TILE) * TILE),
-            dma((3,)), others, others, others, others, reducing, reducing, reducing, reducing,
+            dma((3,)), others, others, others, others,
+            reducing, reducing, reducing, reducing, reducing, reducing,
             dma((tiles + count,)), dma((count,)), others, others,
         ],
         compiler_params=pltpu.CompilerParams(
-            collective_id=0, has_side_effects=True, vmem_limit_bytes=48 * 2**20
+            collective_id=0, has_side_effects=True, vmem_limit_bytes=62 * 2**20
         ),
         name="ace",
     )(orbitals, block_vectors, kernel[None, :])

time: 112 us -> 108 us (0.964)
  Pallas kernels: 107 us -> 104 us
  local copies, waits for them, and re-layouts: 4.18 us -> 2.64 us
    pallas_call x1, Pallas kernels: 107 us -> 104 us  [ace_of(): pl.pallas_call(functools.partial(ace_kernel, count, groups), out_shape=(j...]
    unnamed x8 -> x4, local copies, waits for them, and re-layouts: 4.18 us -> 2.64 us
where the time goes in v3:
time: 108 us; the launch traced here: 107 us
  Pallas kernels  104 us (96%)
  local copies, waits for them, and re-layouts  2.64 us (2%)
    pallas_call x1, Pallas kernels, ace_of(): pl.pallas_call(functools.partial(ace_kernel, count, groups), out_shape=(j...  104 us
    unnamed x4, local copies, waits for them, and re-layouts  2.64 us

profile of v3, /device:TPU:513, one launch (start us, length us, event | category | flops | bytes accessed | tf_op | source)
XLA Modules:
  0.0 107.5 jit_solution(5686601219577516149)
XLA Ops:
  0.6 104.2 %ace.1 = (bf16[96,3072]{1,0:T(8,128)(2,1)}, bf16[32,3072]{1,0:T(8,128)(2,1)}) custom-call(bf16[96,3072]{1,0:T(8,128)(2,1)} %orbitals_ref.1, bf16[32,3072]{1,0:T(8,128)(2,1)} %block_ref.1, f32[1,3072]{1,0:T(1,128)} %bitcast.1), custom_call_target="tpu_custom_call" | custom-call | tf_op jit(solution)/shard_map/ace/pallas_call | solution.py:444
  104.8 0.0 copy-start
  104.8 2.0 %copy.7 = bf16[96,3072]{1,0:T(8,128)(2,1)} copy(bf16[96,3072]{1,0:T(8,128)(2,1)} %get-tuple-element.4) | data formatting | bytes 1179648
  106.8 0.0 copy-done
  106.8 0.7 copy.8
Async XLA Ops:
  104.8 2.0 %copy-start = (bf16[32,3072]{1,0:T(8,128)(2,1)S(1)}, bf16[32,3072]{1,0:T(8,128)(2,1)}, u32[]{:S(2)}) copy-start(bf16[32,3072]{1,0:T(8,128)(2,1)} %get-tuple-element.5) | copy-start | bytes 589828

commit v4 on v3

--- a/solution.py
+++ b/solution.py
@@ -89,7 +89,13 @@
                 between()
             start = last - per_panel
             upper = jnp.concatenate(done[start:last], axis=0)
-            product = dot_split(split(upper.T), split(upper))
+            high, low = split(upper)
+            product = lax.dot_general(
+                jnp.concatenate([high, high, low], axis=0),
+                jnp.concatenate([high, low, high], axis=0),
+                (((0,), (0,)), ((), ())),
+                preferred_element_type=F32,
+            )
             gone = (lane >= start * SUB) & (lane < last * SUB)
             for r in range(last, count):
                 rows[r] = jnp.where(gone, 0.0, rows[r]) - product[r * SUB : r * SUB + SUB, :]
@@ -111,7 +117,7 @@
 
 def dot_split(left, right):
     (lh, ll), (rh, rl) = left, right
-    return dot(lh, rh) + dot(lh, rl) + dot(ll, rh)
+    return dot(jnp.concatenate([lh, lh, ll], axis=1), jnp.concatenate([rh, rl, rh], axis=0))
 
 
 def remote(src, dst, send, recv, band, ga):
@@ -347,7 +353,8 @@
             at = pl.ds(first, TILE)
             ahead = split(dot_split(inverse, split(work[ours, at])))
             lower = split((ahead[0].astype(F32) + ahead[1].astype(F32)).T)
-            following = factored(work[at, at] - dot_split(lower, ahead))
+            value = work[at, at] - dot_split(lower, ahead)
+            following = factored(value) if k < tiles - 2 else None
             lowers = [lower]
         else:
             lowers = []
@@ -395,7 +402,7 @@
             coupling = split(upper[:, base + cols :].T)
             applied = applied + dot_split(coupling, projector)
         if not ending:
-            inverse = following
+            inverse = factored(value) if following is None else following
     exchange[...] = (-applied).astype(BF16)
 
     blocks = []

time: 108 us -> 100 us (0.926)
  Pallas kernels: 104 us -> 96.5 us
    pallas_call x1, Pallas kernels: 104 us -> 96.5 us  [ace_of(): pl.pallas_call(functools.partial(ace_kernel, count, groups), out_shape=(j...]
where the time goes in v4:
time: 100 us; the launch traced here: 99.8 us
  Pallas kernels  96.5 us (96%)
  local copies, waits for them, and re-layouts  2.64 us (3%)
    pallas_call x1, Pallas kernels, ace_of(): pl.pallas_call(functools.partial(ace_kernel, count, groups), out_shape=(j...  96.5 us
    unnamed x4, local copies, waits for them, and re-layouts  2.64 us

profile of v4, /device:TPU:513, one launch (start us, length us, event | category | flops | bytes accessed | tf_op | source)
XLA Modules:
  0.0 99.8 jit_solution(4034573004881851010)
XLA Ops:
  0.6 96.5 %ace.1 = (bf16[96,3072]{1,0:T(8,128)(2,1)}, bf16[32,3072]{1,0:T(8,128)(2,1)}) custom-call(bf16[96,3072]{1,0:T(8,128)(2,1)} %orbitals_ref.1, bf16[32,3072]{1,0:T(8,128)(2,1)} %block_ref.1, f32[1,3072]{1,0:T(1,128)} %bitcast.1), custom_call_target="tpu_custom_call" | custom-call | tf_op jit(solution)/shard_map/ace/pallas_call | solution.py:451
  97.1 0.0 copy-start
  97.1 2.0 %copy.7 = bf16[96,3072]{1,0:T(8,128)(2,1)} copy(bf16[96,3072]{1,0:T(8,128)(2,1)} %get-tuple-element.4) | data formatting | bytes 1179648
  99.1 0.0 copy-done
  99.1 0.7 copy.8
Async XLA Ops:
  97.1 2.0 %copy-start = (bf16[32,3072]{1,0:T(8,128)(2,1)S(1)}, bf16[32,3072]{1,0:T(8,128)(2,1)}, u32[]{:S(2)}) copy-start(bf16[32,3072]{1,0:T(8,128)(2,1)} %get-tuple-element.5) | copy-start | bytes 589828

commit v5 on v4

--- a/solution.py
+++ b/solution.py
@@ -354,7 +354,7 @@
             ahead = split(dot_split(inverse, split(work[ours, at])))
             lower = split((ahead[0].astype(F32) + ahead[1].astype(F32)).T)
             value = work[at, at] - dot_split(lower, ahead)
-            following = factored(value) if k < tiles - 2 else None
+            following = factored(value) if k < tiles - 4 else None
             lowers = [lower]
         else:
             lowers = []
@@ -373,11 +373,6 @@
         parts = split(upper)
         for i in range(k + 2, tiles):
             lowers.append(split(upper[:, i * TILE - start : (i + 1) * TILE - start].T))
-        for i in range(k + 1, tiles):
-            low = max(i * TILE, start)
-            cut = tuple(part[:, low - start :] for part in parts)
-            at = pl.ds(i * TILE, TILE), pl.ds(low, stop - low)
-            work[at] = work[at] - dot_split(lowers[i - k - 1], cut)
         base = all_rows - start
         projector = tuple(part[:, base : base + cols] for part in parts)
         ace[ours, :] = projector[0]
@@ -396,13 +391,20 @@
                 def _(low=low, high=high, target=target):
                     ace_out[target, mine] = ace[pl.ds(low, high - low), :]
 
+        if not ending and following is None:
+            following = factored(value)
+        for i in range(k + 1, tiles):
+            low = max(i * TILE, start)
+            cut = tuple(part[:, low - start :] for part in parts)
+            at = pl.ds(i * TILE, TILE), pl.ds(low, stop - low)
+            work[at] = work[at] - dot_split(lowers[i - k - 1], cut)
         if k == 0:
             early = inverse, lowers, projector
         else:
             coupling = split(upper[:, base + cols :].T)
             applied = applied + dot_split(coupling, projector)
         if not ending:
-            inverse = factored(value) if following is None else following
+            inverse = following
     exchange[...] = (-applied).astype(BF16)
 
     blocks = []

time: 100 us -> 104 us (1.040)
  Pallas kernels: 96.5 us -> 100 us
    pallas_call x1, Pallas kernels: 96.5 us -> 100 us  [ace_of(): pl.pallas_call(functools.partial(ace_kernel, count, groups), out_shape=(j...]
where the time goes in v5:
time: 104 us; the launch traced here: 103 us
  Pallas kernels  100 us (96%)
  local copies, waits for them, and re-layouts  2.64 us (3%)
    pallas_call x1, Pallas kernels, ace_of(): pl.pallas_call(functools.partial(ace_kernel, count, groups), out_shape=(j...  100 us
    unnamed x4, local copies, waits for them, and re-layouts  2.64 us

profile of v5, /device:TPU:513, one launch (start us, length us, event | category | flops | bytes accessed | tf_op | source)
XLA Modules:
  0.0 103.4 jit_solution(8205084878328898991)
XLA Ops:
  0.6 100.1 %ace.1 = (bf16[96,3072]{1,0:T(8,128)(2,1)}, bf16[32,3072]{1,0:T(8,128)(2,1)}) custom-call(bf16[96,3072]{1,0:T(8,128)(2,1)} %orbitals_ref.1, bf16[32,3072]{1,0:T(8,128)(2,1)} %block_ref.1, f32[1,3072]{1,0:T(1,128)} %bitcast.1), custom_call_target="tpu_custom_call" | custom-call | tf_op jit(solution)/shard_map/ace/pallas_call | solution.py:453
  100.7 0.0 copy-start
  100.7 2.0 %copy.7 = bf16[96,3072]{1,0:T(8,128)(2,1)} copy(bf16[96,3072]{1,0:T(8,128)(2,1)} %get-tuple-element.4) | data formatting | bytes 1179648
  102.7 0.0 copy-done
  102.7 0.7 copy.8
Async XLA Ops:
  100.7 2.0 %copy-start = (bf16[32,3072]{1,0:T(8,128)(2,1)S(1)}, bf16[32,3072]{1,0:T(8,128)(2,1)}, u32[]{:S(2)}) copy-start(bf16[32,3072]{1,0:T(8,128)(2,1)} %get-tuple-element.5) | copy-start | bytes 589828
